TPU v7x, 32 devices: a whole 2x2x4 slice. The times are simulated.
32 devices in a mesh: dp: 4 (over z), mp: 8 (over y, x, core).
Axes of the slice: x: 2, y: 2, z: 4, core: 2. Of those that a mesh axis runs over, the one named last changes fastest.
Arguments:
- inputs: bfloat16 [197, 49152], P(None, ('dp', 'mp')), may hold values from -6 to 6
- cotangent: bfloat16 [197, 49152], P(None, ('dp', 'mp')), may hold values from -1.1953125 to 1.1953125
- w_in: bfloat16 [768, 3072], P('dp', 'mp'), may hold values from -0.21875 to 0.21875
- w_out: bfloat16 [3072, 768], P('mp', 'dp'), may hold values from -0.109375 to 0.109375
- prec_in: float32 [768, 3072], P('dp', 'mp'), may hold values from 0.1 to 2
- prec_out: float32 [3072, 768], P('mp', 'dp'), may hold values from 0.1 to 2
Outputs:
- new_prec_in: float32 [768, 3072], P('dp', 'mp')
- new_prec_out: float32 [3072, 768], P('mp', 'dp')
- new_w_in: float32 [768, 3072], P('dp', 'mp')
- new_w_out: float32 [3072, 768], P('mp', 'dp')
All inputs are finite; a program needn't handle non-finite values.
Results may differ from a plain program's by a relative error of at most 0.0028.
Values may be sent and summed in bfloat16 or wider, within the bound.
A program may use at most 64 MiB of HBM per device.

v0:
```python
import functools
import jax
import jax.numpy as jnp
from jax import lax
from jax.experimental import pallas as pl
from jax.experimental.pallas import tpu as pltpu
from jax.sharding import PartitionSpec as P


def gelu_tanh(v):
    return jax.nn.gelu(v, approximate=True)


def per_device(inputs, cotangent, w_in, w_out, prec_in, prec_out):
    SEQ = inputs.shape[0]
    D = w_in.shape[0] * lax.axis_size("dp")
    w_in_full, w_out_full = (
        lax.all_gather(w_in, "dp", axis=0, tiled=True),
        lax.all_gather(w_out, "dp", axis=1, tiled=True),
    )
    whole = lax.all_gather(inputs, "mp", axis=1, tiled=True)
    rows3 = whole.reshape(SEQ, -1, D)
    images = rows3.shape[1]
    pre = jnp.einsum("snd,dh->snh", rows3, w_in_full, preferred_element_type=jnp.float32)
    act = gelu_tanh(pre).astype(jnp.bfloat16)
    cot_whole = lax.all_gather(cotangent, "mp", axis=1, tiled=True)
    cot3 = cot_whole.reshape(SEQ, images, D)
    back = jnp.einsum("snd,hd->snh", cot3, w_out_full, preferred_element_type=jnp.float32)
    per_out = jnp.einsum("snh,snd->nhd", act, cot3, preferred_element_type=jnp.float32)
    sum_out = jnp.sum(per_out, 0)
    sq_out = jnp.sum(per_out * per_out, 0)
    delta = jax.vjp(gelu_tanh, pre)[1](back)[0].astype(jnp.bfloat16)
    rows_again = lax.all_gather(inputs, "mp", axis=1, tiled=True).reshape(SEQ, images, D)
    per_in = jnp.einsum("snd,snh->ndh", rows_again, delta, preferred_element_type=jnp.float32)
    sum_in = jnp.sum(per_in, 0)
    sq_in = jnp.sum(per_in * per_in, 0)
    sum_in, sq_in = (
        lax.psum_scatter(sum_in, "dp", scatter_dimension=0, tiled=True),
        lax.psum_scatter(sq_in, "dp", scatter_dimension=0, tiled=True),
    )
    sum_out, sq_out = (
        lax.psum_scatter(sum_out, "dp", scatter_dimension=1, tiled=True),
        lax.psum_scatter(sq_out, "dp", scatter_dimension=1, tiled=True),
    )
    scale = 1.0 / (images * lax.axis_size("dp"))
    new_prec_in = 0.6 * prec_in + 0.4 * sq_in * scale
    new_prec_out = 0.6 * prec_out + 0.4 * sq_out * scale
    w_in_own = w_in.astype(jnp.float32)
    w_out_own = w_out.astype(jnp.float32)
    new_w_in = w_in_own - 1.0 * (sum_in * scale + 0.1 * w_in_own) / (new_prec_in + 0.1)
    new_w_out = w_out_own - 1.0 * (sum_out * scale + 0.1 * w_out_own) / (new_prec_out + 0.1)
    return (new_prec_in, new_prec_out, new_w_in, new_w_out)


F32, BF16 = jnp.float32, jnp.bfloat16
NT = (((1,), (1,)), ((), ()))
MESH = pl.DeviceIdType.MESH


def dot(a, b):
    return jnp.dot(a, b, preferred_element_type=F32)


def dot_nt(a, b):
    return lax.dot_general(a, b, NT, preferred_element_type=F32)


def kernel(
    x_hbm, c_hbm, win_ref, wout_t_ref, sums_in, sums_out,
    xg, cg, wg_in, wg_out, w_in_t, w_out_f, act, slope, back, delta,
    acc, own, stage, recv, passing, joined,
    loc, ici_s, ici_r, d2d_s, d2d_r, w_s, w_r, rs_s, rs_r, pass_r,
):
    z, m = lax.axis_index("dp"), lax.axis_index("mp")
    core, q = lax.rem(m, 2), m // 2
    xx, yy = lax.rem(q, 2), q // 2
    chips = [yy * 2 + xx, yy * 2 + 1 - xx, (1 - yy) * 2 + xx, (1 - yy) * 2 + 1 - xx]
    same = [2 * chip + core for chip in chips]
    other = [2 * chip + 1 - core for chip in chips]
    xn, yn, partner_id = same[1], same[2], other[0]
    depth = win_ref.shape[0]
    width = 4 * depth
    lo = -(-depth // 128) * 128
    hi = 3 * depth // 128 * 128
    ranges = ((0, lo), (hi, width), (lo, hi))
    images = xg.shape[0]

    def view(p, mm):
        if p < 2:
            return xg.at[2 * mm + p]
        left, right = ranges[(p - 2) // 2]
        return cg.at[2 * mm + (p - 2) % 2, :, pl.ds(left, right - left)]

    def remote(p, mm, to, ssem, rsem):
        return pltpu.make_async_remote_copy(
            src_ref=view(p, mm), dst_ref=view(p, mm), send_sem=ssem, recv_sem=rsem,
            device_id=(z, to), device_id_type=MESH,
        )

    def to_x(p):
        return remote(p, m, xn, ici_s.at[p, 0], ici_r.at[p, 0])

    def to_y(p):
        return remote(p, m, yn, ici_s.at[p, 1], ici_r.at[p, 1])

    def relayed(p):
        first = p % 2 == 0
        return remote(p, same[1 if first else 2], yn if first else xn, ici_s.at[p, 2], ici_r.at[p, 2])

    def across(p, s):
        return remote(p, same[s], partner_id, d2d_s.at[p, s], d2d_r.at[p, s])

    def arrived(p, s):
        remote(p, same[s], xn, ici_s.at[p, 0], ici_r.at[p, s - 1]).wait_recv()

    def from_partner(pieces, s):
        for p in pieces:
            remote(p, other[s], partner_id, d2d_s.at[p, s], d2d_r.at[p, s]).wait_recv()

    def own_sends(even, odd):
        for a, b in ((even, odd),):
            for p in a:
                to_x(p).start()
            for p in b:
                to_y(p).start()
            for p in b:
                to_x(p).start()
            for p in a:
                to_y(p).start()

    def relay(even, odd):
        for p in even:
            arrived(p, 1)
            relayed(p).start()
        for p in odd:
            arrived(p, 2)
            relayed(p).start()
        for p in even:
            across(p, 1).start()
        for p in odd:
            across(p, 2).start()

    def second(even, odd):
        for p in odd:
            arrived(p, 1)
            across(p, 1).start()
        for p in even:
            arrived(p, 2)
            across(p, 2).start()

    def third(even, odd):
        for p in even + odd:
            arrived(p, 3)
            across(p, 3).start()

    x_even, x_odd = [0], [1]
    a_even, a_odd = [2, 4], [3, 5]
    b_even, b_odd = [6], [7]

    locals_ = []
    for i in range(2):
        cols = pl.ds(i * width, width)
        locals_.append(pltpu.make_async_copy(x_hbm.at[:, cols], xg.at[2 * m + i], loc.at[i]))
    for i in range(2):
        cols = pl.ds(i * width, width)
        locals_.append(pltpu.make_async_copy(c_hbm.at[:, cols], cg.at[2 * m + i], loc.at[2 + i]))
    for copy in locals_:
        copy.start()

    barrier = pltpu.get_barrier_semaphore()
    zs = [lax.rem(z + o, 4) for o in (1, 2, 3)]
    peers = [(z, xn), (z, yn), (z, partner_id)] + [(there, m) for there in zs]
    for peer in peers:
        pl.semaphore_signal(barrier, inc=1, device_id=peer, device_id_type=MESH)
    pl.semaphore_wait(barrier, len(peers))

    locals_[0].wait()
    locals_[1].wait()
    own_sends(x_even, x_odd)
    for p in x_even + x_odd:
        across(p, 0).start()

    rows = pl.ds(pl.multiple_of(z * depth, 16), depth)

    def weight(k, o):
        src, dst = ((win_ref, wg_in), (wout_t_ref, wg_out))[k]
        return pltpu.make_async_remote_copy(
            src_ref=src, dst_ref=dst.at[rows], send_sem=w_s.at[k, o], recv_sem=w_r.at[k, o],
            device_id=(zs[o], m), device_id_type=MESH,
        )

    for k in range(2):
        for o in range(3):
            weight(k, o).start()
    locals_[2].wait()
    locals_[3].wait()
    for p in a_even + a_odd + b_even + b_odd:
        across(p, 0).start()
    wg_in[rows, :] = win_ref[...]
    wg_out[rows, :] = wout_t_ref[...]
    acc[...] = jnp.zeros_like(acc)

    def forward(chip):
        def one(j, carry):
            n = 4 * chip + j
            pre = dot_nt(w_in_t[...], xg[n])
            square = pre * pre
            t = jnp.tanh(0.7978845608028654 * pre * (1.0 + 0.044715 * square))
            half = 0.5 * (1.0 + t)
            act[n] = (pre * half).astype(BF16)
            slope[n] = half + 0.5 * pre * (1.0 - t * t) * (0.7978845608028654 * (1.0 + 0.134145 * square))
            return carry
        lax.fori_loop(0, 4, one, 0)

    def accumulate(lhs, rhs, first, count, span):
        cols = slice(*span)
        gs = [dot(lhs[first + j], rhs[first + j, :, cols]) for j in range(count)]
        total, squares = gs[0], gs[0] * gs[0]
        for g in gs[1:]:
            total, squares = total + g, squares + g * g
        acc[0, :, cols] += total
        acc[1, :, cols] += squares

    def chunk_a(chip):
        def pair(h, carry):
            first = 4 * chip + 2 * h
            for j in range(2):
                n = first + j
                back[n] = dot_nt(w_out_f[:, 0:lo], cg[n, :, 0:lo]) + dot_nt(w_out_f[:, hi:width], cg[n, :, hi:width])
            for span in ranges[:2]:
                accumulate(act, cg, first, 2, span)
            return carry
        lax.fori_loop(0, 2, pair, 0)

    def chunk_b(chip):
        def pair(h, carry):
            first = 4 * chip + 2 * h
            for j in range(2):
                n = first + j
                whole = back[n] + dot_nt(w_out_f[:, lo:hi], cg[n, :, lo:hi])
                delta[n] = (whole * slope[n]).astype(BF16)
            accumulate(act, cg, first, 2, ranges[2])
            return carry
        lax.fori_loop(0, 2, pair, 0)

    def settle(part, span):
        cols = slice(*span)
        for a in range(2):
            turned = acc[a, :, cols].T
            own[part, a, cols, :] = turned
            stage[part, a, cols, :] = turned.astype(BF16)
            if part == 0:
                acc[a, :, cols] = jnp.zeros_like(acc[a, :, cols])

    def block(part, j):
        return stage.at[part, :, pl.ds(j * depth, depth), :]

    def place(j):
        inner = j in (1, 2)
        return (1 - j, 3, 2, 1 - int(inner)) if j < 2 else (5 - j, 0, 1, 1 - int(inner))

    def near_copy(part, j):
        return pltpu.make_async_remote_copy(
            src_ref=block(part, j), dst_ref=recv.at[part, 0],
            send_sem=rs_s.at[part, j], recv_sem=rs_r.at[part, 0],
            device_id=(j, m), device_id_type=MESH,
        )

    def pass_copy(part, j):
        _, _, far_inner, kind = place(j)
        return pltpu.make_async_remote_copy(
            src_ref=block(part, j), dst_ref=passing.at[part, kind],
            send_sem=rs_s.at[part, j], recv_sem=pass_r.at[part, kind],
            device_id=(far_inner, m), device_id_type=MESH,
        )

    def joined_copy(part, j):
        kind = place(j)[3]
        return pltpu.make_async_remote_copy(
            src_ref=joined.at[part, kind], dst_ref=recv.at[part, 1],
            send_sem=rs_s.at[part, j], recv_sem=rs_r.at[part, 1],
            device_id=(j, m), device_id_type=MESH,
        )

    def give(part, targets):
        for j in targets:
            mate, far_end, _, _ = place(j)

            @pl.when(z == mate)
            def _():
                near_copy(part, j).start()

            @pl.when(z == far_end)
            def _():
                pass_copy(part, j).start()

    def combine(part, targets):
        for j in targets:
            _, _, far_inner, kind = place(j)

            @pl.when(z == far_inner)
            def _():
                pass_copy(part, j).wait_recv()
                for a in range(2):
                    mine = own[part, a, j * depth:(j + 1) * depth, :]
                    joined[part, kind, a] = (mine + passing[part, kind, a].astype(F32)).astype(BF16)
                joined_copy(part, j).start()

    relay(x_even, x_odd)
    own_sends(a_even, a_odd)
    for o in range(3):
        weight(0, o).wait_recv()
    w_in_t[...] = wg_in[...].astype(F32).T.astype(BF16)
    from_partner([0, 1], 0)
    forward(chips[0])
    second(x_even, x_odd)
    from_partner([0, 1], 1)
    forward(chips[1])
    from_partner([0, 1], 2)
    forward(chips[2])
    third(x_even, x_odd)
    from_partner([0, 1], 3)
    forward(chips[3])

    for o in range(3):
        weight(1, o).wait_recv()
    w_out_f[...] = wg_out[...].astype(F32).T.astype(BF16)
    pieces = a_even + a_odd
    relay(a_even, a_odd)
    own_sends(b_even, b_odd)
    from_partner(pieces, 0)
    chunk_a(chips[0])
    second(a_even, a_odd)
    from_partner(pieces, 1)
    chunk_a(chips[1])
    from_partner(pieces, 2)
    chunk_a(chips[2])
    third(a_even, a_odd)
    relay(b_even, b_odd)
    from_partner(pieces, 3)
    chunk_a(chips[3])
    settle(0, ranges[0])
    give(0, [0])
    settle(0, ranges[1])
    give(0, [3])

    pieces = b_even + b_odd
    from_partner(pieces, 0)
    chunk_b(chips[0])
    second(b_even, b_odd)
    from_partner(pieces, 1)
    chunk_b(chips[1])
    from_partner(pieces, 2)
    chunk_b(chips[2])
    third(b_even, b_odd)
    from_partner(pieces, 3)
    chunk_b(chips[3])
    settle(0, ranges[2])
    give(0, [1, 2])
    combine(0, [0, 3])

    for span, targets in zip(ranges, ([0], [3], [1, 2])):
        def four(k, carry, span=span):
            accumulate(delta, xg, 4 * k, 4, span)
            return carry
        lax.fori_loop(0, images // 4, four, 0)
        settle(1, span)
        give(1, targets)
        if span == ranges[0]:
            combine(0, [1, 2])
    combine(1, [0, 3, 1, 2])

    def collected(part, sums):
        near_copy(part, 0).wait_recv()
        joined_copy(part, 0).wait_recv()
        for a in range(2):
            total = own[part, a, rows, :]
            for t in range(2):
                total = total + recv[part, t, a].astype(F32)
            sums[a] = total

    collected(0, sums_out)
    collected(1, sums_in)

    for p in range(8):
        to_x(p).wait_send()
        to_y(p).wait_send()
        relayed(p).wait_send()
        for s in range(4):
            across(p, s).wait_send()
    for k in range(2):
        for o in range(3):
            weight(k, o).wait_send()
    for part in range(2):
        for j in range(4):
            @pl.when(z != j)
            def _():
                near_copy(part, j).wait_send()


def fused(inputs, cotangent, w_in, w_out, prec_in, prec_out):
    seq, local = inputs.shape
    depth, hid = w_in.shape
    width = 4 * depth
    images = 8 * local // width
    vmem, hbm = pl.BlockSpec(memory_space=pltpu.VMEM), pl.BlockSpec(memory_space=pl.ANY)
    dma = pltpu.SemaphoreType.DMA
    sums_in, sums_out = pl.pallas_call(
        kernel,
        out_shape=[jax.ShapeDtypeStruct((2, depth, hid), F32)] * 2,
        in_specs=[hbm, hbm] + [vmem] * 2,
        out_specs=[vmem] * 2,
        scratch_shapes=[
            pltpu.VMEM((images, seq, width), BF16),
            pltpu.VMEM((images, seq, width), BF16),
            pltpu.VMEM((width, hid), BF16),
            pltpu.VMEM((width, hid), BF16),
            pltpu.VMEM((hid, width), BF16),
            pltpu.VMEM((hid, width), BF16),
            pltpu.VMEM((images, hid, seq), BF16),
            pltpu.VMEM((images, hid, seq), F32),
            pltpu.VMEM((images, hid, seq), F32),
            pltpu.VMEM((images, hid, seq), BF16),
            pltpu.VMEM((2, hid, width), F32),
            pltpu.VMEM((2, 2, width, hid), F32),
            pltpu.VMEM((2, 2, width, hid), BF16),
            pltpu.VMEM((2, 2, 2, depth, hid), BF16),
            pltpu.VMEM((2, 2, 2, depth, hid), BF16),
            pltpu.VMEM((2, 2, 2, depth, hid), BF16),
            dma((4,)), dma((8, 3)), dma((8, 3)), dma((8, 4)), dma((8, 4)),
            dma((2, 3)), dma((2, 3)), dma((2, 4)), dma((2, 2)), dma((2, 2)),
        ],
        compiler_params=pltpu.CompilerParams(
            collective_id=0, has_side_effects=True, vmem_limit_bytes=60 * 1024 * 1024
        ),
    )(inputs, cotangent, w_in, w_out.T)

    scale = 1.0 / (images * 4)

    def updated(sums, prec, w):
        new_prec = 0.6 * prec + 0.4 * sums[1] * scale
        mean = w.astype(F32)
        return new_prec, mean - 1.0 * (sums[0] * scale + 0.1 * mean) / (new_prec + 0.1)

    new_prec_in, new_w_in = updated(sums_in, prec_in, w_in)
    new_prec_out, new_w_out = updated(sums_out, prec_out.T, w_out.T)
    return new_prec_in, new_prec_out.T, new_w_in, new_w_out.T


def solution(mesh):
    placed = (
        P(None, ("dp", "mp")),
        P(None, ("dp", "mp")),
        P("dp", "mp"),
        P("mp", "dp"),
        P("dp", "mp"),
        P("mp", "dp"),
    )
    body = fused if dict(mesh.shape) == {"dp": 4, "mp": 8} else per_device
    return jax.shard_map(
        body,
        mesh=mesh,
        in_specs=placed,
        out_specs=(P("dp", "mp"), P("mp", "dp"), P("dp", "mp"), P("mp", "dp")),
        check_vma=False,
    )
```

profile of v0, /device:TPU:16, one launch (start us, length us, event | category | flops | bytes accessed | tf_op | source)
XLA Modules:
  0.0 95.9 jit_solution(6279083276622509704)
XLA Ops:
  0.6 0.0 copy-start
  0.6 0.0 copy-start.1
  0.7 0.0 copy-start.2
  0.7 0.0 copy-start.3
  0.7 92.8 %shard_map.93 = (f32[2,192,384]{2,1,0:T(8,128)}, f32[2,192,384]{2,1,0:T(8,128)}) custom-call(bf16[197,1536]{1,0:T(8,128)(2,1)} %x_hbm.1, bf16[197,1536]{1,0:T(8,128)(2,1)} %c_hbm.1, bf16[192,384]{1,0:T(8,128)(2,1)} %win_ref.1, bf16[192,384]{1,0:T(8,128)(2,1)} %bitcast.25), custom_call_target="tpu_custom_call" | custom-call | tf_op jit(solution)/shard_map/pallas_call | solution.py:408
  93.5 0.0 copy-done
  93.5 0.0 copy-done.1
  93.5 0.0 copy-done.2
  93.5 0.0 copy-done.3
  93.6 2.3 %convert_subtract_fusion.1 = (f32[192,384]{1,0:T(8,128)}, f32[192,384]{1,0:T(8,128)}, f32[384,192]{0,1:T(8,128)}, f32[384,192]{0,1:T(8,128)}) fusion(bf16[192,384]{1,0:T(8,128)(2,1)S(1)} %copy-done, f32[2,192,384]{2,1,0:T(8,128)} %get-tuple-element.6, f32[192,384]{1,0:T(8,128)S(1)} %copy-done.2, f32[2,192,384]{2,1,0:T(8,128)} %get-tuple-element.7, ...), kind=kLoop, calls=%fused_computation.2 | loop fusion | flops 1474560 | bytes 3244032 | tf_op jit(solution)/shard_map/sub | solution.py:443
Async XLA Ops:
  0.6 92.9 %copy-start = (bf16[192,384]{1,0:T(8,128)(2,1)S(1)}, bf16[192,384]{1,0:T(8,128)(2,1)}, u32[]{:S(2)}) copy-start(bf16[192,384]{1,0:T(8,128)(2,1)} %win_ref.1) | copy-start | bytes 442372
  0.6 92.9 %copy-start.1 = (bf16[384,192]{0,1:T(8,128)(2,1)S(1)}, bf16[384,192]{0,1:T(8,128)(2,1)}, u32[]{:S(2)}) copy-start(bf16[384,192]{0,1:T(8,128)(2,1)} %param.9) | copy-start | bytes 442372
  0.7 92.9 %copy-start.2 = (f32[192,384]{1,0:T(8,128)S(1)}, f32[192,384]{1,0:T(8,128)}, u32[]{:S(2)}) copy-start(f32[192,384]{1,0:T(8,128)} %param.10) | copy-start | bytes 884740
  0.7 92.9 %copy-start.3 = (f32[384,192]{0,1:T(8,128)S(1)}, f32[384,192]{0,1:T(8,128)}, u32[]{:S(2)}) copy-start(f32[384,192]{0,1:T(8,128)} %param.11) | copy-start | bytes 884740
where the time goes:
time: 96.1 us; the launch traced here: 95.9 us
  Pallas kernels  92.8 us (97%)
  other arithmetic  2.35 us (2%)
    pallas_call x1, Pallas kernels, fused(): pl.pallas_call(kernel, out_shape=[jax.ShapeDtypeStruct((2, depth, hid), F...  92.8 us
    sub x1, other arithmetic, updated(): mean - 1.0 * (sums[0] * scale + 0.1 * mean) / (new_prec + 0.1)  2.35 us

commit v1 on v0

v1 whole, which is shorter than its diff:
```python
import functools
import jax
import jax.numpy as jnp
from jax import lax
from jax.experimental import pallas as pl
from jax.experimental.pallas import tpu as pltpu
from jax.sharding import PartitionSpec as P


def gelu_tanh(v):
    return jax.nn.gelu(v, approximate=True)


def per_device(inputs, cotangent, w_in, w_out, prec_in, prec_out):
    SEQ = inputs.shape[0]
    D = w_in.shape[0] * lax.axis_size("dp")
    w_in_full, w_out_full = (
        lax.all_gather(w_in, "dp", axis=0, tiled=True),
        lax.all_gather(w_out, "dp", axis=1, tiled=True),
    )
    whole = lax.all_gather(inputs, "mp", axis=1, tiled=True)
    rows3 = whole.reshape(SEQ, -1, D)
    images = rows3.shape[1]
    pre = jnp.einsum("snd,dh->snh", rows3, w_in_full, preferred_element_type=jnp.float32)
    act = gelu_tanh(pre).astype(jnp.bfloat16)
    cot_whole = lax.all_gather(cotangent, "mp", axis=1, tiled=True)
    cot3 = cot_whole.reshape(SEQ, images, D)
    back = jnp.einsum("snd,hd->snh", cot3, w_out_full, preferred_element_type=jnp.float32)
    per_out = jnp.einsum("snh,snd->nhd", act, cot3, preferred_element_type=jnp.float32)
    sum_out = jnp.sum(per_out, 0)
    sq_out = jnp.sum(per_out * per_out, 0)
    delta = jax.vjp(gelu_tanh, pre)[1](back)[0].astype(jnp.bfloat16)
    rows_again = lax.all_gather(inputs, "mp", axis=1, tiled=True).reshape(SEQ, images, D)
    per_in = jnp.einsum("snd,snh->ndh", rows_again, delta, preferred_element_type=jnp.float32)
    sum_in = jnp.sum(per_in, 0)
    sq_in = jnp.sum(per_in * per_in, 0)
    sum_in, sq_in = (
        lax.psum_scatter(sum_in, "dp", scatter_dimension=0, tiled=True),
        lax.psum_scatter(sq_in, "dp", scatter_dimension=0, tiled=True),
    )
    sum_out, sq_out = (
        lax.psum_scatter(sum_out, "dp", scatter_dimension=1, tiled=True),
        lax.psum_scatter(sq_out, "dp", scatter_dimension=1, tiled=True),
    )
    scale = 1.0 / (images * lax.axis_size("dp"))
    new_prec_in = 0.6 * prec_in + 0.4 * sq_in * scale
    new_prec_out = 0.6 * prec_out + 0.4 * sq_out * scale
    w_in_own = w_in.astype(jnp.float32)
    w_out_own = w_out.astype(jnp.float32)
    new_w_in = w_in_own - 1.0 * (sum_in * scale + 0.1 * w_in_own) / (new_prec_in + 0.1)
    new_w_out = w_out_own - 1.0 * (sum_out * scale + 0.1 * w_out_own) / (new_prec_out + 0.1)
    return (new_prec_in, new_prec_out, new_w_in, new_w_out)


F32, BF16 = jnp.float32, jnp.bfloat16
NT = (((1,), (1,)), ((), ()))
MESH = pl.DeviceIdType.MESH
LANES = 128


def dot(a, b):
    return jnp.dot(a, b, preferred_element_type=F32)


def dot_nt(a, b):
    return lax.dot_general(a, b, NT, preferred_element_type=F32)


def kernel(
    x_hbm, c_hbm, win_ref, wout_t_ref, sums_in, sums_out,
    xg, cg, wg_in, wg_out, w_in_t, w_out_f, act, slope, back, delta,
    acc, own, stage, recv, passing, joined,
    loc, ici_s, ici_r, d2d_s, d2d_r, own_s, own_r, w_s, w_r, rs_s, rs_r, pass_r,
):
    z, m = lax.axis_index("dp"), lax.axis_index("mp")
    core, q = lax.rem(m, 2), m // 2
    xx, yy = lax.rem(q, 2), q // 2
    side, inner = z // 2, lax.rem((z + 1) // 2, 2)
    z_near = z + 1 - 2 * lax.rem(z, 2)

    def chip_at(s):
        return lax.rem(xx + lax.rem(s, 2), 2) + 2 * lax.rem(yy + s // 2, 2)

    chips = [chip_at(s) for s in range(4)]
    same = [2 * chip + core for chip in chips]
    other = [2 * chip + 1 - core for chip in chips]
    xn, yn, partner_id = same[1], same[2], other[0]
    depth = win_ref.shape[0]
    width = 4 * depth
    tiles = width // LANES
    x_pair = (0, 1)

    def flipped(start, size, whole, way):
        return whole - size - start + way * (2 * start + size - whole)

    def columns(start, size):
        return pl.ds(pl.multiple_of(flipped(start, size, width, side), LANES), size)

    def pair_of(k):
        return (2 + 2 * k, 3 + 2 * k)

    def view(p, mm):
        if p < 2:
            return xg.at[2 * mm + p]
        return cg.at[2 * mm + p % 2, :, columns((p - 2) // 2 * LANES, LANES)]

    def remote(src, to, ssem, rsem):
        return pltpu.make_async_remote_copy(
            src_ref=src, dst_ref=src, send_sem=ssem, recv_sem=rsem,
            device_id=(z, to), device_id_type=MESH,
        )

    def to_x(p):
        return remote(view(p, m), xn, ici_s.at[p, 0], ici_r.at[p, 0])

    def to_y(p):
        return remote(view(p, m), yn, ici_s.at[p, 1], ici_r.at[p, 1])

    def relayed(p):
        first = p % 2 == 0
        return remote(view(p, same[1 if first else 2]), yn if first else xn, ici_s.at[p, 2], ici_r.at[p, 2])

    def across(p, s):
        return remote(view(p, same[s]), partner_id, d2d_s.at[p, s - 1], d2d_r.at[p, s - 1])

    def whole_across(k, mm):
        return remote((xg, cg)[k // 2].at[2 * mm + k % 2], partner_id, own_s.at[k], own_r.at[k])

    def arrived(p, s):
        remote(view(p, same[s]), xn, ici_s.at[p, 0], ici_r.at[p, s - 1]).wait_recv()

    def from_partner(pair, s):
        for p in pair:
            remote(view(p, other[s]), partner_id, d2d_s.at[p, s - 1], d2d_r.at[p, s - 1]).wait_recv()

    def send_first(pair):
        to_x(pair[0]).start()
        to_y(pair[1]).start()

    def send_second(pair):
        to_x(pair[1]).start()
        to_y(pair[0]).start()

    def relay(pair):
        arrived(pair[0], 1)
        relayed(pair[0]).start()
        arrived(pair[1], 2)
        relayed(pair[1]).start()

    def relay_across(pair):
        across(pair[0], 1).start()
        across(pair[1], 2).start()

    def second(pair):
        arrived(pair[1], 1)
        across(pair[1], 1).start()
        arrived(pair[0], 2)
        across(pair[0], 2).start()

    def third(pair):
        for p in pair:
            arrived(p, 3)
            across(p, 3).start()

    locals_ = []
    for k in range(4):
        src, dst = ((x_hbm, xg), (c_hbm, cg))[k // 2]
        cols = pl.ds(k % 2 * width, width)
        locals_.append(pltpu.make_async_copy(src.at[:, cols], dst.at[2 * m + k % 2], loc.at[k]))
    for copy in locals_:
        copy.start()

    barrier = pltpu.get_barrier_semaphore()
    zs = [lax.rem(z + o, 4) for o in (1, 2, 3)]
    peers = [(z, xn), (z, yn), (z, partner_id)] + [(there, m) for there in zs]
    for peer in peers:
        pl.semaphore_signal(barrier, inc=1, device_id=peer, device_id_type=MESH)
    pl.semaphore_wait(barrier, len(peers))

    locals_[0].wait()
    locals_[1].wait()
    send_first(x_pair)
    send_second(x_pair)
    for k in range(2):
        whole_across(k, m).start()

    rows = pl.ds(pl.multiple_of(z * depth, 16), depth)

    def weight(k, o):
        src, dst = ((win_ref, wg_in), (wout_t_ref, wg_out))[k]
        return pltpu.make_async_remote_copy(
            src_ref=src, dst_ref=dst.at[rows], send_sem=w_s.at[k, o], recv_sem=w_r.at[k, o],
            device_id=(zs[o], m), device_id_type=MESH,
        )

    for k in range(2):
        for o in range(3):
            weight(k, o).start()
    locals_[2].wait()
    locals_[3].wait()
    send_first(pair_of(0))
    for k in range(2, 4):
        whole_across(k, m).start()
    wg_in[rows, :] = win_ref[...]
    wg_out[rows, :] = wout_t_ref[...]

    def forward(s, first, count):
        def one(j, carry):
            n = 4 * chips[s] + j
            pre = dot_nt(w_in_t[...], xg[n])
            square = pre * pre
            t = jnp.tanh(0.7978845608028654 * pre * (1.0 + 0.044715 * square))
            half = 0.5 * (1.0 + t)
            act[n] = (pre * half).astype(BF16)
            slope[n] = half + 0.5 * pre * (1.0 - t * t) * (0.7978845608028654 * (1.0 + 0.134145 * square))
            return carry
        lax.fori_loop(first, first + count, one, 0)

    def gradients(part, lhs, rhs, n, cols, fresh):
        gs = [dot(lhs[n + j], rhs[n + j, :, cols]) for j in range(4)]
        total, squares = gs[0], gs[0] * gs[0]
        for g in gs[1:]:
            total, squares = total + g, squares + g * g
        if fresh:
            acc[part, 0, :, cols] = total
            acc[part, 1, :, cols] = squares
        else:
            acc[part, 0, :, cols] += total
            acc[part, 1, :, cols] += squares

    def own_gradients(part, lhs, rhs):
        def one(k, carry):
            cols = pl.ds(pl.multiple_of(k * 2 * LANES, LANES), 2 * LANES)
            gradients(part, lhs, rhs, 4 * chips[0], cols, True)
            return carry
        lax.fori_loop(0, tiles // 2, one, 0)

    def far_gradients(part, lhs, rhs, cols):
        def one(s, carry):
            gradients(part, lhs, rhs, 4 * chip_at(s), cols, False)
            return carry
        lax.fori_loop(1, 4, one, 0)

    def backward(n, cols, fresh, last):
        for j in range(4):
            whole = dot_nt(w_out_f[:, cols], cg[n + j, :, cols])
            if not fresh:
                whole = back[n + j] + whole
            if last:
                delta[n + j] = (whole * slope[n + j]).astype(BF16)
            else:
                back[n + j] = whole

    def far_backward(k, last, sources=(1, 4)):
        cols = columns(2 * k * LANES, 2 * LANES)

        def one(s, carry):
            backward(4 * chip_at(s), cols, k == 0, last)
            return carry
        lax.fori_loop(*sources, one, 0)

    def settle(part, start, size):
        cols = columns(start, size)
        for a in range(2):
            turned = acc[part, a, :, cols].T
            own[part, a, cols, :] = turned
            stage[part, a, cols, :] = turned.astype(BF16)

    cuts = sorted({k * LANES for k in range(tiles + 1)} | {j * depth for j in range(5)})
    blocks = [(start, end - start, start // depth) for start, end in zip(cuts, cuts[1:])]

    def in_chunk(b, way):
        start, size, at = blocks[b]
        return pl.ds(pl.multiple_of(flipped(start - at * depth, size, depth, way), 16), size)

    def in_width(b):
        start, size, _ = blocks[b]
        return pl.ds(pl.multiple_of(flipped(start, size, width, side), 16), size)

    def pass_copy(part, b):
        at = blocks[b][2]
        return pltpu.make_async_remote_copy(
            src_ref=stage.at[part, :, in_width(b), :], dst_ref=passing.at[part, at, :, in_chunk(b, side), :],
            send_sem=rs_s.at[part, b], recv_sem=pass_r.at[part, b],
            device_id=(z_near, m), device_id_type=MESH,
        )

    def near_copy(part, b):
        return pltpu.make_async_remote_copy(
            src_ref=stage.at[part, :, in_width(b), :], dst_ref=recv.at[part, 0, :, in_chunk(b, side), :],
            send_sem=rs_s.at[part, b], recv_sem=rs_r.at[part, b],
            device_id=(z_near, m), device_id_type=MESH,
        )

    def joined_copy(part, b, way):
        at = blocks[b][2]
        return pltpu.make_async_remote_copy(
            src_ref=joined.at[part, at, :, in_chunk(b, side), :], dst_ref=recv.at[part, 1, :, in_chunk(b, way), :],
            send_sem=rs_s.at[part, b], recv_sem=rs_r.at[part, b],
            device_id=(3 * (1 - side) if at == 0 else 2 - side, m), device_id_type=MESH,
        )

    def inside(start, end):
        return [b for b, (first, _, _) in enumerate(blocks) if start <= first < end]

    def give(part, start, end):
        for b in inside(start, end):
            at = blocks[b][2]

            @pl.when(inner == (1 if at == 3 else 0))
            def _():
                (pass_copy if at < 2 else near_copy)(part, b).start()

    def combine(part, start, end):
        for b in inside(start, end):
            at = blocks[b][2]

            @pl.when(inner == 1)
            def _():
                pass_copy(part, b).wait_recv()
                here = in_chunk(b, side)
                for a in range(2):
                    mine = own[part, a, in_width(b), :]
                    joined[part, at, a, here, :] = (mine + passing[part, at, a, here, :].astype(F32)).astype(BF16)
                joined_copy(part, b, side).start()

    def out_step(k):
        far_gradients(0, act, cg, columns(k * LANES, LANES))
        settle(0, k * LANES, LANES)
        give(0, k * LANES, (k + 1) * LANES)

    def at_tile(k):
        return k * LANES, (k + 1) * LANES

    p0, p1, p2, p3, p4, p5 = [pair_of(k) for k in range(tiles)]

    relay(x_pair)
    send_second(p0)
    relay_across(x_pair)
    for o in range(3):
        weight(0, o).wait_recv()
    w_in_t[...] = wg_in[...].astype(F32).T.astype(BF16)
    for k in range(2):
        whole_across(k, other[0]).wait_recv()
    forward(0, 0, 4)
    for k in range(2, 4):
        whole_across(k, other[0]).wait_recv()
    own_gradients(0, act, cg)
    second(x_pair)
    relay(p0)
    send_first(p1)
    send_second(p1)
    send_first(p2)
    send_second(p2)
    relay_across(p0)
    from_partner(x_pair, 1)
    forward(1, 0, 4)
    from_partner(x_pair, 2)
    forward(2, 0, 4)
    third(x_pair)
    second(p0)
    from_partner(x_pair, 3)
    forward(3, 0, 2)
    third(p0)
    forward(3, 2, 2)
    relay(p1)
    send_first(p3)
    send_second(p3)
    relay_across(p1)
    for s in range(1, 4):
        from_partner(p0, s)
    out_step(0)
    second(p1)

    for o in range(3):
        weight(1, o).wait_recv()
    w_out_f[...] = wg_out[...].astype(F32).T.astype(BF16)
    backward(4 * chips[0], pl.ds(0, width), True, True)
    relay(p2)
    send_first(p4)
    send_second(p4)
    relay_across(p2)
    second(p2)
    third(p1)
    for s in range(1, 4):
        from_partner(p1, s)
    out_step(1)
    relay(p3)
    send_first(p5)
    send_second(p5)
    relay_across(p3)
    far_backward(0, False)
    second(p3)
    third(p2)
    combine(0, *at_tile(0))
    for s in range(1, 4):
        from_partner(p2, s)
    out_step(2)
    relay(p4)
    relay_across(p4)
    second(p4)
    own_gradients(1, delta, xg)
    third(p3)
    combine(0, *at_tile(1))
    relay(p5)
    relay_across(p5)
    for s in range(1, 4):
        from_partner(p3, s)
    out_step(3)
    far_backward(1, False)
    second(p5)
    third(p4)
    combine(0, *at_tile(2))
    third(p5)
    for s in range(1, 4):
        from_partner(p4, s)
    out_step(4)
    for s in range(1, 3):
        from_partner(p5, s)
    far_backward(2, True, (1, 3))
    from_partner(p5, 3)
    far_backward(2, True, (3, 4))

    for k in range(tiles // 2):
        start, size = 2 * k * LANES, 2 * LANES
        far_gradients(1, delta, xg, columns(start, size))
        settle(1, start, size)
        give(1, start, start + size)
        if k == 0:
            out_step(5)

    def collected(part, sums):
        for near, joint, kind in (((6, 7), (0, 1), 0), ((4, 5), (2, 3), 1)):
            @pl.when(inner == kind)
            def _():
                for b in near:
                    near_copy(part, b).wait_recv()
                for b in joint:
                    joined_copy(part, b, 1 - side).wait_recv()
        for a in range(2):
            total = own[part, a, rows, :]
            for t in range(2):
                total = total + recv[part, t, a].astype(F32)
            sums[a] = total

    collected(0, sums_out)
    combine(1, 0, 2 * depth)
    collected(1, sums_in)

    for pair in (x_pair, p0, p1, p2, p3, p4, p5):
        for p in pair:
            to_x(p).wait_send()
            to_y(p).wait_send()
            relayed(p).wait_send()
            for s in range(1, 4):
                across(p, s).wait_send()
    for k in range(4):
        whole_across(k, m).wait_send()
    for k in range(2):
        for o in range(3):
            weight(k, o).wait_send()
    for part in range(2):
        for b in range(len(blocks)):
            at = blocks[b][2]
            if at < 2:
                pass_copy(part, b).wait_send()
            else:
                @pl.when(inner == (1 if at == 3 else 0))
                def _():
                    near_copy(part, b).wait_send()


def fused(inputs, cotangent, w_in, w_out, prec_in, prec_out):
    seq, local = inputs.shape
    depth, hid = w_in.shape
    width = 4 * depth
    images = 8 * local // width
    pieces = 2 + 2 * width // LANES
    vmem, hbm = pl.BlockSpec(memory_space=pltpu.VMEM), pl.BlockSpec(memory_space=pl.ANY)
    dma = pltpu.SemaphoreType.DMA
    sums_in, sums_out = pl.pallas_call(
        kernel,
        out_shape=[jax.ShapeDtypeStruct((2, depth, hid), F32)] * 2,
        in_specs=[hbm, hbm] + [vmem] * 2,
        out_specs=[vmem] * 2,
        scratch_shapes=[
            pltpu.VMEM((images, seq, width), BF16),
            pltpu.VMEM((images, seq, width), BF16),
            pltpu.VMEM((width, hid), BF16),
            pltpu.VMEM((width, hid), BF16),
            pltpu.VMEM((hid, width), BF16),
            pltpu.VMEM((hid, width), BF16),
            pltpu.VMEM((images, hid, seq), BF16),
            pltpu.VMEM((images, hid, seq), F32),
            pltpu.VMEM((images, hid, seq), F32),
            pltpu.VMEM((images, hid, seq), BF16),
            pltpu.VMEM((2, 2, hid, width), F32),
            pltpu.VMEM((2, 2, width, hid), F32),
            pltpu.VMEM((2, 2, width, hid), BF16),
            pltpu.VMEM((2, 2, 2, depth, hid), BF16),
            pltpu.VMEM((2, 2, 2, depth, hid), BF16),
            pltpu.VMEM((2, 2, 2, depth, hid), BF16),
            dma((4,)), dma((pieces, 3)), dma((pieces, 3)), dma((pieces, 3)), dma((pieces, 3)),
            dma((4,)), dma((4,)), dma((2, 3)), dma((2, 3)), dma((2, 8)), dma((2, 8)), dma((2, 4)),
        ],
        compiler_params=pltpu.CompilerParams(
            collective_id=0, has_side_effects=True, vmem_limit_bytes=60 * 1024 * 1024
        ),
    )(inputs, cotangent, w_in, w_out.T)

    scale = 1.0 / (images * 4)

    def updated(sums, prec, w):
        new_prec = 0.6 * prec + 0.4 * sums[1] * scale
        mean = w.astype(F32)
        return new_prec, mean - 1.0 * (sums[0] * scale + 0.1 * mean) / (new_prec + 0.1)

    new_prec_in, new_w_in = updated(sums_in, prec_in, w_in)
    new_prec_out, new_w_out = updated(sums_out, prec_out.T, w_out.T)
    return new_prec_in, new_prec_out.T, new_w_in, new_w_out.T


def solution(mesh):
    placed = (
        P(None, ("dp", "mp")),
        P(None, ("dp", "mp")),
        P("dp", "mp"),
        P("mp", "dp"),
        P("dp", "mp"),
        P("mp", "dp"),
    )
    body = fused if dict(mesh.shape) == {"dp": 4, "mp": 8} else per_device
    return jax.shard_map(
        body,
        mesh=mesh,
        in_specs=placed,
        out_specs=(P("dp", "mp"), P("mp", "dp"), P("dp", "mp"), P("mp", "dp")),
        check_vma=False,
    )
```

time: 96.1 us -> 86.3 us (0.90)
  the two profiles are of different devices: /device:TPU:16 before, /device:TPU:0 now
where the time goes in v1:
time: 86.3 us; the launch traced here: 85.1 us
  Pallas kernels  82.1 us (95%)
  other arithmetic  2.35 us (3%)
    pallas_call x1, Pallas kernels, fused(): pl.pallas_call(kernel, out_shape=[jax.ShapeDtypeStruct((2, depth, hid), F...  82.1 us
    sub x1, other arithmetic, updated(): mean - 1.0 * (sums[0] * scale + 0.1 * mean) / (new_prec + 0.1)  2.35 us

profile of v1, /device:TPU:0, one launch (start us, length us, event | category | flops | bytes accessed | tf_op | source)
XLA Modules:
  0.0 85.1 jit_solution(10223287588015683061)
XLA Ops:
  0.6 0.0 copy-start
  0.6 0.0 copy-start.1
  0.7 0.0 copy-start.2
  0.7 0.0 copy-start.3
  0.7 82.1 %shard_map.93 = (f32[2,192,384]{2,1,0:T(8,128)}, f32[2,192,384]{2,1,0:T(8,128)}) custom-call(bf16[197,1536]{1,0:T(8,128)(2,1)} %x_hbm.1, bf16[197,1536]{1,0:T(8,128)(2,1)} %c_hbm.1, bf16[192,384]{1,0:T(8,128)(2,1)} %win_ref.1, bf16[192,384]{1,0:T(8,128)(2,1)} %bitcast.25), custom_call_target="tpu_custom_call" | custom-call | tf_op jit(solution)/shard_map/pallas_call | solution.py:481
  82.7 0.0 copy-done
  82.8 0.0 copy-done.1
  82.8 0.0 copy-done.2
  82.8 0.0 copy-done.3
  82.8 2.3 %convert_subtract_fusion.1 = (f32[192,384]{1,0:T(8,128)}, f32[192,384]{1,0:T(8,128)}, f32[384,192]{0,1:T(8,128)}, f32[384,192]{0,1:T(8,128)}) fusion(bf16[192,384]{1,0:T(8,128)(2,1)S(1)} %copy-done, f32[2,192,384]{2,1,0:T(8,128)} %get-tuple-element.6, f32[192,384]{1,0:T(8,128)S(1)} %copy-done.2, f32[2,192,384]{2,1,0:T(8,128)} %get-tuple-element.7, ...), kind=kLoop, calls=%fused_computation.2 | loop fusion | flops 1474560 | bytes 3244032 | tf_op jit(solution)/shard_map/sub | solution.py:516
Async XLA Ops:
  0.6 82.1 %copy-start = (bf16[192,384]{1,0:T(8,128)(2,1)S(1)}, bf16[192,384]{1,0:T(8,128)(2,1)}, u32[]{:S(2)}) copy-start(bf16[192,384]{1,0:T(8,128)(2,1)} %win_ref.1) | copy-start | bytes 442372
  0.6 82.1 %copy-start.1 = (bf16[384,192]{0,1:T(8,128)(2,1)S(1)}, bf16[384,192]{0,1:T(8,128)(2,1)}, u32[]{:S(2)}) copy-start(bf16[384,192]{0,1:T(8,128)(2,1)} %param.9) | copy-start | bytes 442372
  0.7 82.1 %copy-start.2 = (f32[192,384]{1,0:T(8,128)S(1)}, f32[192,384]{1,0:T(8,128)}, u32[]{:S(2)}) copy-start(f32[192,384]{1,0:T(8,128)} %param.10) | copy-start | bytes 884740
  0.7 82.1 %copy-start.3 = (f32[384,192]{0,1:T(8,128)S(1)}, f32[384,192]{0,1:T(8,128)}, u32[]{:S(2)}) copy-start(f32[384,192]{0,1:T(8,128)} %param.11) | copy-start | bytes 884740
